TPU v7x, 32 devices: a whole 2x2x4 slice. The times are simulated.
32 devices in a mesh: dp: 2 (over x), ctx: 4 (over y, core), tp: 4 (over z).
Axes of the slice: x: 2, y: 2, z: 4, core: 2. Of those that a mesh axis runs over, the one named last changes fastest.
Arguments:
- block_input: bfloat16 [2, 8, 256, 2048], P('dp', 'ctx', 'tp'), may hold values from -6 to 6
- block_order: int32 [2, 8], P('dp'), may hold values from 0 to 7, each once within a row
- w_qkv: bfloat16 [2048, 3, 2048], P(('dp', 'ctx'), None, 'tp'), may hold values from -1 to 1
- w_out: bfloat16 [2048, 2048], P('tp', ('dp', 'ctx')), may hold values from -3 to 3
- gain_attn: bfloat16 [2048], P(('dp', 'ctx')), may hold values from 0.5 to 1.5
- w_gate_up: bfloat16 [2048, 2, 8192], P(('dp', 'ctx'), None, 'tp'), may hold values from -0.125 to 0.125
- w_down: bfloat16 [8192, 2048], P('tp', ('dp', 'ctx')), may hold values from -0.0625 to 0.0625
- gain_mlp: bfloat16 [2048], P(('dp', 'ctx')), may hold values from 0.5 to 1.5
- cotangent: bfloat16 [2, 8, 256, 2048], P('dp', 'ctx', 'tp'), may hold values from -6 to 6
Outputs:
- block_output: bfloat16 [2, 8, 256, 2048], P('dp', 'ctx', 'tp')
- input_grad: float32 [2, 8, 256, 2048], P('dp', 'ctx', 'tp')
- grad_qkv: float32 [2048, 3, 2048], P(('dp', 'ctx'), None, 'tp')
- grad_out: float32 [2048, 2048], P('tp', ('dp', 'ctx'))
- grad_gain_attn: float32 [2048], P(('dp', 'ctx'))
- grad_gate_up: float32 [2048, 2, 8192], P(('dp', 'ctx'), None, 'tp')
- grad_down: float32 [8192, 2048], P('tp', ('dp', 'ctx'))
- grad_gain_mlp: float32 [2048], P(('dp', 'ctx'))
Inputs may be any that keep to these rules, and one draw needn't show every extreme that they name: `block_order`: each row lists every block number of one sequence once.
All inputs are finite; a program needn't handle non-finite values.
Results may differ from a plain program's by a relative error of at most 0.019.
Values may be sent and summed in bfloat16 or wider, within the bound.
A program may use at most 192 MiB of HBM per device.

v0:
```python
import jax
import jax.numpy as jnp
from jax import lax
from jax.sharding import PartitionSpec as P

HEAD_DIM = 64
EPSILON = 1e-05
ROPE_BASE = 130000.0
NEG_LARGE = -1e30


def rope_tables(positions, head_size):
    half = head_size // 2
    freq = ROPE_BASE ** (-(jnp.arange(half, dtype=jnp.float32) * 2.0 / head_size))
    angle = positions.astype(jnp.float32)[..., None] * freq
    cosine = jnp.cos(angle)
    sine = jnp.sin(angle)
    return (jnp.concatenate([cosine, cosine], -1), jnp.concatenate([sine, sine], -1))


def rotate(values):
    half = values.shape[-1] // 2
    return jnp.concatenate([-values[..., half:], values[..., :half]], -1)


def unrotate(values):
    half = values.shape[-1] // 2
    return jnp.concatenate([values[..., half:], -values[..., :half]], -1)


def rope_apply(values, cosine, sine):
    return values * cosine + rotate(values) * sine


def rope_back(grads, cosine, sine):
    return grads * cosine + unrotate(grads * sine)


def gather_rows(values):
    return lax.all_gather(values, "tp", axis=2, tiled=True)


def sum_rows(values):
    return lax.psum_scatter(values, "tp", scatter_dimension=2, tiled=True)


def gather_cotangent(values):
    return lax.all_gather(values, "tp", axis=2, tiled=True)


def sum_normed(values):
    return lax.psum_scatter(values, "tp", scatter_dimension=2, tiled=True)


def block_scores(query, key_blk, query_pos, key_pos, head_count):
    key_heads = key_blk.reshape(key_blk.shape[0], head_count, HEAD_DIM)
    scores = jnp.einsum("qhe,khe->hqk", query, key_heads, preferred_element_type=jnp.float32)
    visible = key_pos[None, :] <= query_pos[:, None]
    return jnp.where(visible[None], scores, -jnp.inf)


def online_update(state, query, query_pos, key_blk, value_blk, key_pos, head_count):
    run_max, run_sum, run_acc = state
    scores = block_scores(query, key_blk, query_pos, key_pos, head_count)
    new_max = jnp.maximum(run_max, jnp.max(scores, -1))
    factor = jnp.exp(run_max - new_max)
    probs = jnp.exp(scores - new_max[..., None])
    new_sum = run_sum * factor + jnp.sum(probs, -1)
    value_heads = value_blk.reshape(value_blk.shape[0], head_count, HEAD_DIM).astype(jnp.float32)
    mixed = jnp.einsum("hqk,khe->qhe", probs, value_heads, precision=lax.Precision.HIGHEST)
    new_acc = run_acc * factor.T[:, :, None] + mixed
    return (new_max, new_sum, new_acc)


def backward_block(
    query, query_pos, grad_blk, log_total, delta, key_blk, value_blk, key_pos, head_count
):
    scores = block_scores(query, key_blk, query_pos, key_pos, head_count)
    probs = jnp.exp(scores - log_total[..., None])
    value_heads = value_blk.reshape(value_blk.shape[0], head_count, HEAD_DIM)
    key_heads = key_blk.reshape(key_blk.shape[0], head_count, HEAD_DIM)
    dprobs = jnp.einsum("qhe,khe->hqk", grad_blk, value_heads, preferred_element_type=jnp.float32)
    grad_scores = (probs * (dprobs - delta[..., None])).astype(jnp.bfloat16)
    grad_query = jnp.einsum(
        "hqk,khe->qhe", grad_scores, key_heads, preferred_element_type=jnp.float32
    )
    grad_key = jnp.einsum("hqk,qhe->khe", grad_scores, query, preferred_element_type=jnp.float32)
    grad_value = jnp.einsum(
        "hqk,qhe->khe", probs.astype(jnp.bfloat16), grad_blk, preferred_element_type=jnp.float32
    )
    flat_width = head_count * HEAD_DIM
    return (grad_query, grad_key.reshape(-1, flat_width), grad_value.reshape(-1, flat_width))


def body(block_input, block_order, w_qkv, w_out, gain_attn, w_gate_up, w_down, gain_mlp, cotangent):
    f32 = jnp.float32
    bf16 = jnp.bfloat16
    seq_count = block_input.shape[0]
    row_count = block_input.shape[2]
    span = row_count * lax.axis_size("tp")
    local_width = w_qkv.shape[2]
    head_count = local_width // HEAD_DIM
    query_rows = 2 * span
    block_total = block_order.shape[1]
    ctx_index = lax.axis_index("ctx")
    my_ids = lax.dynamic_slice_in_dim(block_order, ctx_index * 2, 2, 1)
    offsets = jnp.arange(span, dtype=jnp.int32)
    query_pos = (my_ids[:, :, None] * span + offsets).reshape(seq_count, query_rows)
    cosine, sine = rope_tables(query_pos, HEAD_DIM)
    cosine = cosine[:, :, None, :]
    sine = sine[:, :, None, :]
    full_qkv, full_out, full_gain_attn = (
        lax.all_gather(w_qkv, ("dp", "ctx"), axis=0, tiled=True),
        lax.all_gather(w_out, ("dp", "ctx"), axis=1, tiled=True),
        lax.all_gather(gain_attn, ("dp", "ctx"), axis=0, tiled=True),
    )
    x_float = block_input.astype(f32)
    rms_attn = lax.rsqrt(jnp.mean(x_float * x_float, -1, keepdims=True) + EPSILON)
    unit_attn = x_float * rms_attn
    normed_attn = (unit_attn * full_gain_attn.astype(f32)).astype(bf16)
    normed_attn_full = gather_rows(normed_attn)
    qkv = jnp.einsum("spcd,dte->spcte", normed_attn_full, full_qkv, preferred_element_type=f32)
    qkv = qkv.reshape(seq_count, query_rows, 3, head_count, HEAD_DIM)
    queries = (rope_apply(qkv[:, :, 0], cosine, sine) * 0.125).astype(bf16)
    keys = rope_apply(qkv[:, :, 1], cosine, sine).astype(bf16)
    values = qkv[:, :, 2].astype(bf16)
    key_send = keys.reshape(seq_count, 2, span, local_width)
    value_send = values.reshape(seq_count, 2, span, local_width)
    initial = (
        jnp.full((seq_count, head_count, query_rows), NEG_LARGE, f32),
        jnp.zeros((seq_count, head_count, query_rows), f32),
        jnp.zeros((seq_count, query_rows, head_count, HEAD_DIM), f32),
    )
    key_piece = lax.all_gather(key_send, "ctx", axis=1, tiled=True)
    value_piece = lax.all_gather(value_send, "ctx", axis=1, tiled=True)

    def visit(step_index, inner):
        run_max, run_sum, run_acc = inner
        key_ids = lax.dynamic_index_in_dim(block_order, step_index, 1, False)
        key_blk = lax.dynamic_index_in_dim(key_piece, step_index, 1, False)
        value_blk = lax.dynamic_index_in_dim(value_piece, step_index, 1, False)
        member = 0
        key_pos = key_ids[member] * span + offsets
        operands = (run_max[member], run_sum[member], run_acc[member])

        def update(current, member=member, key_pos=key_pos):
            return online_update(
                current,
                queries[member],
                query_pos[member],
                key_blk[member],
                value_blk[member],
                key_pos,
                head_count,
            )

        result = update(operands)
        maxes = [result[0]]
        sums = [result[1]]
        accs = [result[2]]
        return (jnp.stack(maxes), jnp.stack(sums), jnp.stack(accs))

    run_max, run_sum, run_acc = lax.fori_loop(0, key_piece.shape[1], visit, initial)
    attention = (run_acc / jnp.transpose(run_sum, (0, 2, 1))[..., None]).astype(bf16)
    log_total = run_max + jnp.log(run_sum)
    attn_flat = attention.reshape(seq_count, 2, span, local_width)
    attn_part = jnp.einsum("spce,ed->spcd", attn_flat, full_out, preferred_element_type=f32)
    resid_mid = x_float + sum_rows(attn_part)
    full_gate_up, full_down, full_gain_mlp = (
        lax.all_gather(w_gate_up, ("dp", "ctx"), axis=0, tiled=True),
        lax.all_gather(w_down, ("dp", "ctx"), axis=1, tiled=True),
        lax.all_gather(gain_mlp, ("dp", "ctx"), axis=0, tiled=True),
    )
    rms_mlp = lax.rsqrt(jnp.mean(resid_mid * resid_mid, -1, keepdims=True) + EPSILON)
    unit_mlp = resid_mid * rms_mlp
    normed_mlp = (unit_mlp * full_gain_mlp.astype(f32)).astype(bf16)
    normed_mlp_full = gather_rows(normed_mlp)
    gate_up = jnp.einsum(
        "spcd,dtf->spctf", normed_mlp_full, full_gate_up, preferred_element_type=f32
    )
    gate = gate_up[:, :, :, 0]
    upper = gate_up[:, :, :, 1]
    sigma = jax.nn.sigmoid(gate)
    hidden = (gate * sigma * upper).astype(bf16)
    down_part = jnp.einsum("spcf,fd->spcd", hidden, full_down, preferred_element_type=f32)
    resid_out = resid_mid + sum_rows(down_part)
    block_output = resid_out.astype(bf16)
    back_gate_up, back_down, back_gain_mlp = (full_gate_up, full_down, full_gain_mlp)
    back_qkv, back_out, back_gain_attn = (full_qkv, full_out, full_gain_attn)
    cotan_full = gather_cotangent(cotangent)
    grad_down_local = jnp.einsum("spcf,spcd->fd", hidden, cotan_full, preferred_element_type=f32)
    grad_hidden = jnp.einsum("spcd,fd->spcf", cotan_full, back_down, preferred_element_type=f32)
    act_grad = jnp.stack(
        [grad_hidden * upper * sigma * (1.0 + gate * (1.0 - sigma)), grad_hidden * gate * sigma],
        axis=3,
    ).astype(bf16)
    grad_gate_up_local = jnp.einsum(
        "spcd,spctf->dtf", normed_mlp_full, act_grad, preferred_element_type=f32
    )
    grad_normed_mlp = sum_normed(
        jnp.einsum("spctf,dtf->spcd", act_grad, back_gate_up, preferred_element_type=f32)
    )
    gain_term_mlp = jnp.sum(grad_normed_mlp * unit_mlp, axis=(0, 1, 2))
    scaled_two = grad_normed_mlp * back_gain_mlp.astype(f32)
    grad_mid = cotangent.astype(f32) + rms_mlp * (
        scaled_two - unit_mlp * jnp.mean(scaled_two * unit_mlp, -1, keepdims=True)
    )
    mlp_shares = (
        lax.psum_scatter(
            grad_gate_up_local.astype(jnp.bfloat16), ("dp", "ctx"), scatter_dimension=0, tiled=True
        ).astype(jnp.float32),
        lax.psum_scatter(
            grad_down_local.astype(jnp.bfloat16), ("dp", "ctx"), scatter_dimension=1, tiled=True
        ).astype(jnp.float32),
        lax.psum_scatter(
            gain_term_mlp.astype(jnp.bfloat16), ("dp", "ctx"), scatter_dimension=0, tiled=True
        ).astype(jnp.float32),
    )
    grad_mid_b = grad_mid.astype(bf16)
    mid_full = gather_cotangent(grad_mid_b)
    grad_out_local = jnp.einsum("spce,spcd->ed", attn_flat, mid_full, preferred_element_type=f32)
    grad_attention = jnp.einsum(
        "spcd,ed->spce", mid_full, back_out, preferred_element_type=f32
    ).astype(bf16)
    grad_attention = grad_attention.reshape(seq_count, query_rows, head_count, HEAD_DIM)
    delta = jnp.transpose(
        jnp.sum(grad_attention.astype(f32) * attention.astype(f32), -1), (0, 2, 1)
    )
    all_keys, all_values = (
        lax.all_gather(key_send, "ctx", axis=1, tiled=True),
        lax.all_gather(value_send, "ctx", axis=1, tiled=True),
    )

    def back_step(grad_queries, slot):
        key_ids = lax.dynamic_index_in_dim(block_order, slot, 1, False)
        key_blk = lax.dynamic_index_in_dim(all_keys, slot, 1, False)
        value_blk = lax.dynamic_index_in_dim(all_values, slot, 1, False)
        member = 0
        key_pos = key_ids[member] * span + offsets

        def work(current, member=member, key_pos=key_pos):
            grad_query, grad_key, grad_value = backward_block(
                queries[member],
                query_pos[member],
                grad_attention[member],
                log_total[member],
                delta[member],
                key_blk[member],
                value_blk[member],
                key_pos,
                head_count,
            )
            return (current + grad_query, grad_key, grad_value)

        result = work(grad_queries[member])
        query_list = [result[0]]
        key_list = [result[1]]
        value_list = [result[2]]
        return (jnp.stack(query_list), (jnp.stack(key_list), jnp.stack(value_list)))

    start_grads = jnp.zeros((seq_count, query_rows, head_count, HEAD_DIM), f32)
    grad_queries, (key_terms, value_terms) = lax.scan(
        back_step, start_grads, jnp.arange(block_total, dtype=jnp.int32)
    )
    grad_keys, grad_values = (
        lax.psum_scatter(
            key_terms.astype(jnp.bfloat16), "ctx", scatter_dimension=0, tiled=True
        ).astype(jnp.float32),
        lax.psum_scatter(
            value_terms.astype(jnp.bfloat16), "ctx", scatter_dimension=0, tiled=True
        ).astype(jnp.float32),
    )
    grad_keys = jnp.transpose(grad_keys, (1, 0, 2, 3)).reshape(
        seq_count, query_rows, head_count, HEAD_DIM
    )
    grad_values = jnp.transpose(grad_values, (1, 0, 2, 3)).reshape(
        seq_count, query_rows, head_count, HEAD_DIM
    )
    qkv_grad = jnp.stack(
        [
            rope_back(grad_queries, cosine, sine) * 0.125,
            rope_back(grad_keys, cosine, sine),
            grad_values,
        ],
        axis=2,
    ).astype(bf16)
    qkv_grad = qkv_grad.reshape(seq_count, 2, span, 3, local_width)
    grad_qkv_local = jnp.einsum(
        "spcd,spcte->dte", normed_attn_full, qkv_grad, preferred_element_type=f32
    )
    grad_normed_attn = sum_normed(
        jnp.einsum("spcte,dte->spcd", qkv_grad, back_qkv, preferred_element_type=f32)
    )
    gain_term_attn = jnp.sum(grad_normed_attn * unit_attn, axis=(0, 1, 2))
    scaled_one = grad_normed_attn * back_gain_attn.astype(f32)
    input_grad = grad_mid + rms_attn * (
        scaled_one - unit_attn * jnp.mean(scaled_one * unit_attn, -1, keepdims=True)
    )
    shard_qkv, shard_out, shard_gain_attn = (
        lax.psum_scatter(
            grad_qkv_local.astype(jnp.bfloat16), ("dp", "ctx"), scatter_dimension=0, tiled=True
        ).astype(jnp.float32),
        lax.psum_scatter(
            grad_out_local.astype(jnp.bfloat16), ("dp", "ctx"), scatter_dimension=1, tiled=True
        ).astype(jnp.float32),
        lax.psum_scatter(
            gain_term_attn.astype(jnp.bfloat16), ("dp", "ctx"), scatter_dimension=0, tiled=True
        ).astype(jnp.float32),
    )
    shard_gate_up, shard_down, shard_gain_mlp = mlp_shares
    total_gain_attn, total_gain_mlp = lax.psum((shard_gain_attn, shard_gain_mlp), "tp")
    return (
        block_output,
        input_grad,
        shard_qkv,
        shard_out,
        total_gain_attn,
        shard_gate_up,
        shard_down,
        total_gain_mlp,
    )


def solution(mesh):
    in_specs = (
        P("dp", "ctx", "tp", None),
        P("dp", None),
        P(("dp", "ctx"), None, "tp"),
        P("tp", ("dp", "ctx")),
        P(("dp", "ctx")),
        P(("dp", "ctx"), None, "tp"),
        P("tp", ("dp", "ctx")),
        P(("dp", "ctx")),
        P("dp", "ctx", "tp", None),
    )
    out_specs = (
        P("dp", "ctx", "tp", None),
        P("dp", "ctx", "tp", None),
        P(("dp", "ctx"), None, "tp"),
        P("tp", ("dp", "ctx")),
        P(("dp", "ctx")),
        P(("dp", "ctx"), None, "tp"),
        P("tp", ("dp", "ctx")),
        P(("dp", "ctx")),
    )
    return jax.shard_map(body, mesh=mesh, in_specs=in_specs, out_specs=out_specs, check_vma=False)
```

profile of v0, /device:TPU:0, one launch (start us, length us, event | category | flops | bytes accessed | tf_op | source)
XLA Modules:
  0.0 1424.0 jit_solution(8658560242486038990)
XLA Ops:
  27.8 30.2 %all-gather.15.cloned.1.call-done = bf16[2048,3,512]{2,0,1:T(8,128)(2,1)} async-done(((bf16[256,3,512]{2,0,1:T(8,128)(2,1)}), bf16[2048,3,512]{2,0,1:T(8,128)(2,1)}) %all-gather.15.cloned.1.call-update) | async-done | bytes 6291472 | tf_op jit(solution)/shard_map/all_gather | solution.py:113
  66.9 39.0 %all-gather.13.cloned.1.call-done = bf16[1,2,256,2048]{3,2,1,0:T(8,128)(2,1)} async-done(((bf16[1,2,64,2048]{3,2,1,0:T(8,128)(2,1)}), bf16[1,2,256,2048]{3,2,1,0:T(8,128)(2,1)}) %all-gather.13.cloned.1.call-update) | async-done | bytes 2097168 | tf_op jit(solution)/shard_map/all_gather | solution.py:40
  133.6 15.4 %all-gather.17.cloned.1.call-done = bf16[1,8,256,512]{3,2,0,1:T(8,128)(2,1)} async-done(((bf16[1,2,256,512]{3,2,0,1:T(8,128)(2,1)}), bf16[1,8,256,512]{3,2,0,1:T(8,128)(2,1)}) %all-gather.17.cloned.1.call-update) | async-done | bytes 2097168 | tf_op jit(solution)/shard_map/all_gather | solution.py:134
  152.9 20.7 %all-gather.19.cloned.1.call-done = bf16[1,8,256,512]{3,2,0,1:T(8,128)(2,1)} async-done(((bf16[1,2,256,512]{3,2,0,1:T(8,128)(2,1)}), bf16[1,8,256,512]{3,2,0,1:T(8,128)(2,1)}) %all-gather.19.cloned.1.call-update) | async-done | bytes 2097168 | tf_op jit(solution)/shard_map/all_gather | solution.py:135
  177.6 92.5 %while.34 = (s32[]{:T(128)}, f32[1,8,512]{2,1,0:T(8,128)S(1)}, f32[1,8,512]{2,1,0:T(8,128)S(1)}, f32[1,512,8,64]{1,3,2,0:T(8,128)S(1)}, s32[1,8]{1,0:T(1,128)S(1...) while((s32[]{:T(128)}, f32[1,8,512]{2,1,0:T(8,128)S(1)}, ...), condition=%wide.region_4.5_spmd.clone, body=%wide.region_1.4_spmd.clone.sunk | while | flops 947548928 | bytes 34334904 | solution.py:163
  285.1 67.6 %reduce-scatter.11.cloned.1.call-done = f32[1,2,64,2048]{3,2,1,0:T(8,128)} async-done(((f32[1,2,256,2048]{3,2,1,0:T(8,128)}), f32[1,2,64,2048]{3,2,1,0:T(8,128)}) %reduce-scatter.11.cloned.1.call-update) | async-done | bytes 1048592 | tf_op jit(solution)/shard_map/reduce_scatter | solution.py:44
  361.0 40.7 %all-gather.23.cloned.1.call-done = bf16[1,2,256,2048]{3,2,1,0:T(8,128)(2,1)} async-done(((bf16[1,2,64,2048]{3,2,1,0:T(8,128)(2,1)}), bf16[1,2,256,2048]{3,2,1,0:T(8,128)(2,1)}) %all-gather.23.cloned.1.call-update) | async-done | bytes 2097168 | tf_op jit(solution)/shard_map/all_gather | solution.py:40
  401.7 91.0 %all-gather.25.cloned.1.call-done = bf16[2048,2,2048]{2,0,1:T(8,128)(2,1)} async-done(((bf16[256,2,2048]{2,0,1:T(8,128)(2,1)}), bf16[2048,2,2048]{2,0,1:T(8,128)(2,1)}) %all-gather.25.cloned.1.call-update) | async-done | bytes 16777232 | tf_op jit(solution)/shard_map/all_gather | solution.py:170
  492.7 15.1 %fusion.48 = f32[1,2,256,2,2048]{4,2,3,1,0:T(8,128)} fusion(bf16[2048,2,2048]{2,0,1:T(8,128)(2,1)} %all-gather.25.cloned.1.call-done, bf16[1,2,256,2048]{3,2,1,0:T(8,128)(2,1)} %all-gather.23.cloned.1.call-done), kind=kOutput, calls=%fused_computation.71 | convolution fusion | flops 8589934592 | bytes 27262976 | tf_op jit(solution)/shard_map/spcd,dtf->spctf/dot_general | solution.py:178
  507.8 32.2 %all-gather.29.cloned.1.call-done = bf16[1,2,256,2048]{3,2,1,0:T(8,128)(2,1)} async-done(((bf16[1,2,64,2048]{3,2,1,0:T(8,128)(2,1)}), bf16[1,2,256,2048]{3,2,1,0:T(8,128)(2,1)}) %all-gather.29.cloned.1.call-update) | async-done | bytes 2097168 | tf_op jit(solution)/shard_map/all_gather | solution.py:48
  540.0 56.4 %all-gather.27.cloned.1.call-done = bf16[2048,2048]{1,0:T(8,128)(2,1)} async-done(((bf16[2048,256]{1,0:T(8,128)(2,1)}), bf16[2048,2048]{1,0:T(8,128)(2,1)}) %all-gather.27.cloned.1.call-update) | async-done | bytes 8388624 | tf_op jit(solution)/shard_map/all_gather | solution.py:171
  609.8 13.8 fusion.54
  623.6 76.9 %reduce-scatter.15.cloned.1.call-done = f32[1,2,64,2048]{3,2,1,0:T(8,128)} async-done(((f32[1,2,256,2048]{3,2,1,0:T(8,128)}), f32[1,2,64,2048]{3,2,1,0:T(8,128)}) %reduce-scatter.15.cloned.1.call-update) | async-done | bytes 1048592 | tf_op jit(solution)/shard_map/reduce_scatter | solution.py:52
  704.7 46.0 %all-gather.31.cloned.1.call-done = bf16[1,2,256,2048]{3,2,1,0:T(8,128)(2,1)} async-done(((bf16[1,2,64,2048]{3,2,1,0:T(8,128)(2,1)}), bf16[1,2,256,2048]{3,2,1,0:T(8,128)(2,1)}) %all-gather.31.cloned.1.call-update) | async-done | bytes 2097168 | tf_op jit(solution)/shard_map/all_gather | solution.py:48
  760.7 122.6 %while.35 = (s32[]{:T(128)}, f32[1,512,8,64]{1,3,2,0:T(8,128)}, bf16[8,1,256,512]{3,2,0,1:T(8,128)(2,1)}, bf16[8,1,256,512]{3,2,0,1:T(8,128)(2,1)}, s32[8]{0:T(1...) while((s32[]{:T(128)}, f32[1,512,8,64]{1,3,2,0:T(8,128)}, ...), condition=%wide.wide.region_12.13_spmd.clone, body=%wide.wide.region_11.12_spmd.clone.sunk | while | flops 679871232 | bytes 27977976 | solution.py:262
  927.3 20.3 %reduce-scatter.19.cloned.1.call-done = bf16[2,1,256,512]{3,2,0,1:T(8,128)(2,1)} async-done(((bf16[8,1,256,512]{3,2,0,1:T(8,128)(2,1)}), bf16[2,1,256,512]{3,2,0,1:T(8,128)(2,1)}) %reduce-scatter.19.cloned.1.call-update) | async-done | bytes 524304 | tf_op jit(solution)/shard_map/reduce_scatter | solution.py:269
  978.7 14.6 %bitcast_convert_fusion = bf16[2048,2,2048]{2,0,1:T(8,128)(2,1)} fusion(bf16[2,256,1,2048]{3,1,0,2:T(8,128)(2,1)} %copy-done.35, bf16[2,256,1,2048]{3,1,0,2:T(8,128)(2,1)} %copy-done.34, bf16[1,2,256,2048]{3,2,1,0:T(8,128)(2,1)S(1)} %copy-done.28), kind=kOutput, calls=%fused_computation.58 | convolution fusion | flops 8606711808 | bytes 23068672 | tf_op jit(solution)/shard_map/spcd,spctf->dtf/dot_general | solution.py:197
  995.2 27.0 %reduce-scatter.29.cloned.1.call-done = bf16[2048,256]{1,0:T(8,128)(2,1)} async-done(((bf16[2048,2048]{1,0:T(8,128)(2,1)}), bf16[2048,256]{1,0:T(8,128)(2,1)}) %reduce-scatter.29.cloned.1.call-update) | async-done | bytes 1048592 | tf_op jit(solution)/shard_map/reduce_scatter | solution.py:212
  1024.9 41.6 %reduce-scatter.25.cloned.1.call-done = bf16[512,256]{1,0:T(8,128)(2,1)} async-done(((bf16[512,2048]{1,0:T(8,128)(2,1)}), bf16[512,256]{1,0:T(8,128)(2,1)}) %reduce-scatter.25.cloned.1.call-update) | async-done | bytes 262160 | tf_op jit(solution)/shard_map/reduce_scatter | solution.py:303
  1068.3 77.8 %reduce-scatter.21.cloned.1.call-done = f32[1,2,64,2048]{3,2,1,0:T(8,128)} async-done(((f32[1,2,256,2048]{3,2,1,0:T(8,128)}), f32[1,2,64,2048]{3,2,1,0:T(8,128)}) %reduce-scatter.21.cloned.1.call-update) | async-done | bytes 1048592 | tf_op jit(solution)/shard_map/reduce_scatter | solution.py:52
  1147.7 13.6 all-reduce.3
  1173.9 51.9 %reduce-scatter.13.cloned.1.call-done = f32[1,2,64,2048]{3,2,1,0:T(8,128)} async-done(((f32[1,2,256,2048]{3,2,1,0:T(8,128)}), f32[1,2,64,2048]{3,2,1,0:T(8,128)}) %reduce-scatter.13.cloned.1.call-update) | async-done | bytes 1048592 | tf_op jit(solution)/shard_map/reduce_scatter | solution.py:44
  1228.9 62.4 %reduce-scatter.23.cloned.1.call-done = bf16[256,3,512]{2,0,1:T(8,128)(2,1)} async-done(((bf16[2048,3,512]{2,0,1:T(8,128)(2,1)}), bf16[256,3,512]{2,0,1:T(8,128)(2,1)}) %reduce-scatter.23.cloned.1.call-update) | async-done | bytes 786448 | tf_op jit(solution)/shard_map/reduce_scatter | solution.py:300
  1293.8 117.1 %reduce-scatter.27.cloned.1.call-done = bf16[256,2,2048]{2,0,1:T(8,128)(2,1)} async-done(((bf16[2048,2,2048]{2,0,1:T(8,128)(2,1)}), bf16[256,2,2048]{2,0,1:T(8,128)(2,1)}) %reduce-scatter.27.cloned.1.call-update) | async-done | bytes 2097168 | tf_op jit(solution)/shard_map/reduce_scatter | solution.py:209
  (435 shorter events, 422.9 us)
Async XLA Ops:
  7.2 50.9 %all-gather.15.cloned.1.call-start = ((), (), s32[]{:S(2)}) async-start(), calls=%async_computation.11 | async-start | bytes 7077888 | tf_op jit(solution)/shard_map/all_gather | solution.py:113
  7.9 98.0 %all-gather.13.cloned.1.call-start = ((), (), s32[]{:S(2)}) async-start(), calls=%async_computation.10 | async-start | bytes 2621440 | tf_op jit(solution)/shard_map/all_gather | solution.py:40
  23.0 126.0 %all-gather.17.cloned.1.call-start = ((), (), s32[]{:S(2)}) async-start(), calls=%async_computation.12 | async-start | bytes 2621440 | tf_op jit(solution)/shard_map/all_gather | solution.py:134
  127.5 46.1 %all-gather.19.cloned.1.call-start = ((), (), s32[]{:S(2)}) async-start(), calls=%async_computation.13 | async-start | bytes 2621440 | tf_op jit(solution)/shard_map/all_gather | solution.py:135
  131.1 139.3 %all-gather.21.cloned.1.call-start = ((), (), s32[]{:S(2)}) async-start(), calls=%async_computation.14 | async-start | bytes 2359296 | tf_op jit(solution)/shard_map/all_gather | solution.py:114
  131.7 221.0 %reduce-scatter.11.cloned.1.call-start = ((), (), s32[]{:S(2)}) async-start(), calls=%async_computation.15 | async-start | bytes 5242880 | tf_op jit(solution)/shard_map/reduce_scatter | solution.py:44
  275.5 126.2 %all-gather.23.cloned.1.call-start = ((), (), s32[]{:S(2)}) async-start(), calls=%async_computation.16 | async-start | bytes 2621440 | tf_op jit(solution)/shard_map/all_gather | solution.py:40
  354.2 347.9 %copy-start.1 = (f32[1,2,64,2048]{3,2,1,0:T(8,128)}, f32[1,2,64,2048]{3,2,1,0:T(8,128)S(1)}, u32[]{:S(2)}) copy-start(f32[1,2,64,2048]{3,2,1,0:T(8,128)S(1)} %get-tuple-element.460) | copy-start | bytes 3145732
  355.4 137.4 %all-gather.25.cloned.1.call-start = ((), (), s32[]{:S(2)}) async-start(), calls=%async_computation.17 | async-start | bytes 18874368 | tf_op jit(solution)/shard_map/all_gather | solution.py:170
  359.2 180.8 %all-gather.29.cloned.1.call-start = ((), (), s32[]{:S(2)}) async-start(), calls=%async_computation.20 | async-start | bytes 2621440 | tf_op jit(solution)/shard_map/all_gather | solution.py:48
  360.0 236.4 %all-gather.27.cloned.1.call-start = ((), (), s32[]{:S(2)}) async-start(), calls=%async_computation.18 | async-start | bytes 9437184 | tf_op jit(solution)/shard_map/all_gather | solution.py:171
  360.6 339.9 %reduce-scatter.15.cloned.1.call-start = ((), (), s32[]{:S(2)}) async-start(), calls=%async_computation.21 | async-start | bytes 5242880 | tf_op jit(solution)/shard_map/reduce_scatter | solution.py:52
  623.6 127.2 %all-gather.31.cloned.1.call-start = ((), (), s32[]{:S(2)}) async-start(), calls=%async_computation.22 | async-start | bytes 2621440 | tf_op jit(solution)/shard_map/all_gather | solution.py:48
  704.5 208.9 %reduce-scatter.17.cloned.1.call-start = ((), (), s32[]{:S(2)}) async-start(), calls=%async_computation.23 | async-start | bytes 2621440 | tf_op jit(solution)/shard_map/reduce_scatter | solution.py:266
  883.3 64.3 %reduce-scatter.19.cloned.1.call-start = ((), (), s32[]{:S(2)}) async-start(), calls=%async_computation.24 | async-start | bytes 2621440 | tf_op jit(solution)/shard_map/reduce_scatter | solution.py:269
  883.9 138.4 %reduce-scatter.29.cloned.1.call-start = ((), (), s32[]{:S(2)}) async-start(), calls=%async_computation.29 | async-start | bytes 9437184 | tf_op jit(solution)/shard_map/reduce_scatter | solution.py:212
  893.3 173.2 %reduce-scatter.25.cloned.1.call-start = ((), (), s32[]{:S(2)}) async-start(), calls=%async_computation.27 | async-start | bytes 2359296 | tf_op jit(solution)/shard_map/reduce_scatter | solution.py:303
  898.5 247.6 %reduce-scatter.21.cloned.1.call-start = ((), (), s32[]{:S(2)}) async-start(), calls=%async_computation.25 | async-start | bytes 5242880 | tf_op jit(solution)/shard_map/reduce_scatter | solution.py:52
  956.2 269.6 %reduce-scatter.13.cloned.1.call-start = ((), (), s32[]{:S(2)}) async-start(), calls=%async_computation.19 | async-start | bytes 5242880 | tf_op jit(solution)/shard_map/reduce_scatter | solution.py:44
  969.0 322.3 %reduce-scatter.23.cloned.1.call-start = ((), (), s32[]{:S(2)}) async-start(), calls=%async_computation.26 | async-start | bytes 7077888 | tf_op jit(solution)/shard_map/reduce_scatter | solution.py:300
  977.1 433.8 %reduce-scatter.27.cloned.1.call-start = ((), (), s32[]{:S(2)}) async-start(), calls=%async_computation.28 | async-start | bytes 18874368 | tf_op jit(solution)/shard_map/reduce_scatter | solution.py:209
  993.4 232.4 %copy-start.2 = (f32[1,2,64,2048]{3,2,1,0:T(8,128)S(1)}, f32[1,2,64,2048]{3,2,1,0:T(8,128)}, u32[]{:S(2)}) copy-start(f32[1,2,64,2048]{3,2,1,0:T(8,128)} %copy-done.1) | copy-start | bytes 3145732
  993.4 232.4 %copy-start.7 = (f32[1,2,64,2048]{3,2,1,0:T(8,128)S(1)}, f32[1,2,64,2048]{3,2,1,0:T(8,128)}, u32[]{:S(2)}) copy-start(f32[1,2,64,2048]{3,2,1,0:T(8,128)} %reduce-scatter.15.cloned.1.call-done) | copy-start | bytes 3145732
  993.4 232.4 %copy-start.9 = (bf16[1,2,64,2048]{3,2,1,0:T(8,128)(2,1)S(1)}, bf16[1,2,64,2048]{3,2,1,0:T(8,128)(2,1)}, u32[]{:S(2)}) copy-start(bf16[1,2,64,2048]{3,2,1,0:T(8,128)(2,1)} %param.21) | copy-start | bytes 1572868
  (39 other events, 1022.6 us)
Sparse Core Ops, SparseCore 0:
  9.9 48.1 all-gather.14
  60.2 45.6 all-gather.12
  127.6 21.3 all-gather.16
  151.0 22.5 all-gather.18
  175.3 28.0 all-gather.20
  275.6 77.0 reduce-scatter.10
  355.5 46.1 all-gather.22
  404.2 88.5 all-gather.24
  494.3 45.6 all-gather.28
  541.7 54.6 all-gather.26
  623.7 76.7 reduce-scatter.14
  704.6 46.1 all-gather.30
  883.4 29.9 reduce-scatter.16
  916.4 31.1 reduce-scatter.18
  950.9 71.2 reduce-scatter.28
  1025.3 41.1 reduce-scatter.24
  1069.2 76.7 reduce-scatter.20
  1148.2 77.5 reduce-scatter.12
  1229.2 62.0 reduce-scatter.22
  1294.7 116.1 reduce-scatter.26
where the time goes:
time: 1430 us; the launch traced here: 1420 us
  waiting for transfers between devices  931 us (65%)
  matrix products  222 us (16%)
  local copies, waits for them, and re-layouts  109 us (8%)
  other arithmetic  85.4 us (6%)
  blocking collectives  45.4 us (3%)
  between operations  16 us (1%)
    reduce_scatter x2, waiting for transfers between devices, sum_normed(): return lax.psum_scatter(values, 'tp', scatter_dimension=2, tiled=True)  155 us
    reduce_scatter x2, waiting for transfers between devices, sum_rows(): return lax.psum_scatter(values, 'tp', scatter_dimension=2, tiled=True)  119 us
    reduce_scatter x1, waiting for transfers between devices, body(): lax.psum_scatter(grad_gate_up_local.astype(jnp.bfloat16), ('dp', 'ctx'),...  117 us
    all_gather x1, waiting for transfers between devices, body(): lax.all_gather(w_gate_up, ('dp', 'ctx'), axis=0, tiled=True)  91 us
    all_gather x2, waiting for transfers between devices, gather_rows(): return lax.all_gather(values, 'tp', axis=2, tiled=True)  79.7 us
    all_gather x2, waiting for transfers between devices, gather_cotangent(): return lax.all_gather(values, 'tp', axis=2, tiled=True)  78.2 us
    reduce_scatter x1, waiting for transfers between devices, body(): lax.psum_scatter(grad_qkv_local.astype(jnp.bfloat16), ('dp', 'ctx'), scat...  62.4 us
    all_gather x1, waiting for transfers between devices, body(): lax.all_gather(w_down, ('dp', 'ctx'), axis=1, tiled=True)  56.4 us
  transfers between devices with their start and end apart: 20, of which 19 were waited for; matrix products, arithmetic and copies ran while one was open for 15% of the time, Pallas kernels for 0%

commit v1 on v0

--- a/solution.py
+++ b/solution.py
@@ -2,11 +2,36 @@
 import jax.numpy as jnp
 from jax import lax
 from jax.sharding import PartitionSpec as P
+from jax.lax import axis_index, axis_size, ppermute
 
 HEAD_DIM = 64
 EPSILON = 1e-05
 ROPE_BASE = 130000.0
 NEG_LARGE = -1e30
+
+
+def tables_place(row_data, dim_i):
+    row_data = jnp.moveaxis(row_data, 0, dim_i)
+    u_next = row_data.shape
+    return row_data.reshape(
+        *u_next[:dim_i], u_next[dim_i] * u_next[dim_i + 1], *u_next[dim_i + 2 :]
+    )
+
+
+def thing_register(array_here, mesh_dim):
+    fan = axis_size(mesh_dim)
+    reached = array_here[None]
+    for ii in range(fan.bit_length() - 1):
+        inter = 1 << ii
+        far_arr = range(fan)
+        b_now = map(lambda dd: (dd, dd ^ inter), far_arr)
+        k_now = list(b_now)
+        n_now = ppermute(reached, mesh_dim, k_now)
+        response = jnp.stack([reached, n_now], 0)
+        piece_now = axis_index(mesh_dim)
+        earlier = piece_now >> ii & 1
+        reached = jnp.where(earlier == 0, response, response[::-1]).reshape(-1, *array_here.shape)
+    return reached
 
 
 def rope_tables(positions, head_size):
@@ -37,7 +62,12 @@
 
 
 def gather_rows(values):
-    return lax.all_gather(values, "tp", axis=2, tiled=True)
+
+    def follow_zone(inputs, z, along_dim):
+        v_now = thing_register(inputs, z)
+        return tables_place(v_now, along_dim)
+
+    return follow_zone(values, "tp", 2)
 
 
 def sum_rows(values):

time: 1430 us -> 1380 us (0.965)
  waiting for transfers between devices: 931 us -> 864 us
    ppermute x0 -> x4, waiting for transfers between devices: none -> 110 us  [thing_register(): n_now = ppermute(reached, mesh_dim, k_now)]
    all_gather x2 -> x0, waiting for transfers between devices: 79.7 us -> none  [gather_rows(): return lax.all_gather(values, 'tp', axis=2, tiled=True)]
    all_gather x1, waiting for transfers between devices: 91 us -> 27 us  [body(): lax.all_gather(w_gate_up, ('dp', 'ctx'), axis=0, tiled=True)]
    all_gather x1, waiting for transfers between devices: 30.2 us -> 0.01 us  [body(): lax.all_gather(w_qkv, ('dp', 'ctx'), axis=0, tiled=True)]
    unnamed x80 -> x84, local copies, waits for them, and re-layouts: 29.5 us -> 30 us
  transfers between devices with their start and end apart: 20 -> 22, of which waited for: 19 -> 20; matrix products, arithmetic and copies ran while one was open for 15% -> 16% of each run, Pallas kernels for 0% -> 0%
where the time goes in v1:
time: 1380 us; the launch traced here: 1370 us
  waiting for transfers between devices  864 us (63%)
  matrix products  220 us (16%)
  local copies, waits for them, and re-layouts  113 us (8%)
  other arithmetic  86.5 us (6%)
  blocking collectives  45.8 us (3%)
  loops' own time  16.1 us (1%)
  between operations  16 us (1%)
    reduce_scatter x2, waiting for transfers between devices, sum_normed(): return lax.psum_scatter(values, 'tp', scatter_dimension=2, tiled=True)  154 us
    reduce_scatter x1, waiting for transfers between devices, body(): lax.psum_scatter(grad_gate_up_local.astype(jnp.bfloat16), ('dp', 'ctx'),...  117 us
    reduce_scatter x2, waiting for transfers between devices, sum_rows(): return lax.psum_scatter(values, 'tp', scatter_dimension=2, tiled=True)  114 us
    ppermute x4, waiting for transfers between devices, thing_register(): n_now = ppermute(reached, mesh_dim, k_now)  110 us
    all_gather x2, waiting for transfers between devices, gather_cotangent(): return lax.all_gather(values, 'tp', axis=2, tiled=True)  78.4 us
    reduce_scatter x1, waiting for transfers between devices, body(): lax.psum_scatter(grad_qkv_local.astype(jnp.bfloat16), ('dp', 'ctx'), scat...  62.2 us
    all_gather x1, waiting for transfers between devices, body(): lax.all_gather(w_down, ('dp', 'ctx'), axis=1, tiled=True)  56.6 us
    reduce_scatter x1, waiting for transfers between devices, body(): lax.psum_scatter(grad_out_local.astype(jnp.bfloat16), ('dp', 'ctx'), scat...  41.6 us
  transfers between devices with their start and end apart: 22, of which 20 were waited for; matrix products, arithmetic and copies ran while one was open for 16% of the time, Pallas kernels for 0%

profile of v1, /device:TPU:0, one launch (start us, length us, event | category | flops | bytes accessed | tf_op | source)
XLA Modules:
  0.0 1372.1 jit_solution(13812420750441696035)
XLA Ops:
  43.1 41.3 %collective-permute-done.1 = bf16[2,1,2,64,2048]{4,3,2,0,1:T(8,128)(2,1)} collective-permute-done((bf16[2,1,2,64,2048]{4,3,2,0,1:T(8,128)(2,1)S(1)}, bf16[2,1,2,64,2048]{4,3,2,0,1:T(8,128)(2,1)}, u32[]{:S(2)}, u32[]{:S(2)}) %collective-permute-start.1) | collective-permute-done | bytes 1048608 | tf_op jit(solution)/shard_map/ppermute | solution.py:29
  124.5 16.9 %all-gather.13.cloned.1.call-done = bf16[1,8,256,512]{3,2,0,1:T(8,128)(2,1)} async-done(((bf16[1,2,256,512]{3,2,0,1:T(8,128)(2,1)}), bf16[1,8,256,512]{3,2,0,1:T(8,128)(2,1)}) %all-gather.13.cloned.1.call-update) | async-done | bytes 2097168 | tf_op jit(solution)/shard_map/all_gather | solution.py:164
  145.3 20.8 %all-gather.15.cloned.1.call-done = bf16[1,8,256,512]{3,2,0,1:T(8,128)(2,1)} async-done(((bf16[1,2,256,512]{3,2,0,1:T(8,128)(2,1)}), bf16[1,8,256,512]{3,2,0,1:T(8,128)(2,1)}) %all-gather.15.cloned.1.call-update) | async-done | bytes 2097168 | tf_op jit(solution)/shard_map/all_gather | solution.py:165
  170.1 92.6 %while.34 = (s32[]{:T(128)}, f32[1,8,512]{2,1,0:T(8,128)S(1)}, f32[1,8,512]{2,1,0:T(8,128)S(1)}, f32[1,512,8,64]{1,3,2,0:T(8,128)S(1)}, s32[1,8]{1,0:T(1,128)S(1...) while((s32[]{:T(128)}, f32[1,8,512]{2,1,0:T(8,128)S(1)}, ...), condition=%wide.region_4.5_spmd.clone, body=%wide.region_1.4_spmd.clone.sunk | while | flops 947548928 | bytes 34334904 | solution.py:193
  283.0 62.4 %reduce-scatter.11.cloned.1.call-done = f32[1,2,64,2048]{3,2,1,0:T(8,128)} async-done(((f32[1,2,256,2048]{3,2,1,0:T(8,128)}), f32[1,2,64,2048]{3,2,1,0:T(8,128)}) %reduce-scatter.11.cloned.1.call-update) | async-done | bytes 1048592 | tf_op jit(solution)/shard_map/reduce_scatter | solution.py:74
  364.0 44.7 %collective-permute-done.3 = bf16[2,1,2,64,2048]{4,3,2,0,1:T(8,128)(2,1)S(1)} collective-permute-done((bf16[2,1,2,64,2048]{4,3,2,0,1:T(8,128)(2,1)S(1)}, bf16[2,1,2,64,2048]{4,3,2,0,1:T(8,128)(2,1)S(1)}, u32[]{:S(2)}, u32[]{:S(2)}) %collective-permute-start.3) | collective-permute-done | bytes 1048608 | tf_op jit(solution)/shard_map/ppermute | solution.py:29
  411.0 27.0 %all-gather.19.cloned.1.call-done = bf16[2048,2,2048]{2,0,1:T(8,128)(2,1)} async-done(((bf16[256,2,2048]{2,0,1:T(8,128)(2,1)}), bf16[2048,2,2048]{2,0,1:T(8,128)(2,1)}) %all-gather.19.cloned.1.call-update) | async-done | bytes 16777232 | tf_op jit(solution)/shard_map/all_gather | solution.py:200
  438.0 15.1 %fusion.48 = f32[1,2,256,2,2048]{4,2,3,1,0:T(8,128)} fusion(bf16[2,256,2048,1]{2,1,3,0:T(8,128)(2,1)} %bitcast.463, bf16[2048,2,2048]{2,0,1:T(8,128)(2,1)} %all-gather.19.cloned.1.call-done), kind=kOutput, calls=%fused_computation.71 | convolution fusion | flops 8589934592 | bytes 27262976 | tf_op jit(solution)/shard_map/spcd,dtf->spctf/dot_general | solution.py:208
  453.0 32.2 %all-gather.23.cloned.1.call-done = bf16[1,2,256,2048]{3,2,1,0:T(8,128)(2,1)} async-done(((bf16[1,2,64,2048]{3,2,1,0:T(8,128)(2,1)}), bf16[1,2,256,2048]{3,2,1,0:T(8,128)(2,1)}) %all-gather.23.cloned.1.call-update) | async-done | bytes 2097168 | tf_op jit(solution)/shard_map/all_gather | solution.py:78
  485.2 56.6 %all-gather.21.cloned.1.call-done = bf16[2048,2048]{1,0:T(8,128)(2,1)} async-done(((bf16[2048,256]{1,0:T(8,128)(2,1)}), bf16[2048,2048]{1,0:T(8,128)(2,1)}) %all-gather.21.cloned.1.call-update) | async-done | bytes 8388624 | tf_op jit(solution)/shard_map/all_gather | solution.py:201
  555.1 13.8 %fusion.54 = f32[1,2,256,2048]{3,2,1,0:T(8,128)} fusion(bf16[2048,2,2048]{2,0,1:T(8,128)(2,1)} %all-gather.19.cloned.1.call-done, bf16[2,256,1,2048]{3,1,0,2:T(8,128)(2,1)S(1)} %get-tuple-element.470, bf16[2,256,1,2048]{3,1,0,2:T(8,128)(2,1)S(1)} %get-tuple-element.469), kind=kOutput, calls=%fused_computation.81 | convolution fusion | flops 8592031744 | bytes 25165824 | tf_op jit(solution)/shard_map/spctf,dtf->spcd/dot_general | solution.py:231
  569.1 76.7 %reduce-scatter.15.cloned.1.call-done = f32[1,2,64,2048]{3,2,1,0:T(8,128)} async-done(((f32[1,2,256,2048]{3,2,1,0:T(8,128)}), f32[1,2,64,2048]{3,2,1,0:T(8,128)}) %reduce-scatter.15.cloned.1.call-update) | async-done | bytes 1048592 | tf_op jit(solution)/shard_map/reduce_scatter | solution.py:82
  648.8 46.2 %all-gather.25.cloned.1.call-done = bf16[1,2,256,2048]{3,2,1,0:T(8,128)(2,1)} async-done(((bf16[1,2,64,2048]{3,2,1,0:T(8,128)(2,1)}), bf16[1,2,256,2048]{3,2,1,0:T(8,128)(2,1)}) %all-gather.25.cloned.1.call-update) | async-done | bytes 2097168 | tf_op jit(solution)/shard_map/all_gather | solution.py:78
  704.9 126.4 %while.35 = (s32[]{:T(128)}, f32[1,512,8,64]{1,3,2,0:T(8,128)}, bf16[8,1,256,512]{3,2,0,1:T(8,128)(2,1)}, bf16[8,1,256,512]{3,2,0,1:T(8,128)(2,1)}, s32[8]{0:T(1...) while((s32[]{:T(128)}, f32[1,512,8,64]{1,3,2,0:T(8,128)}, ...), condition=%wide.wide.region_12.13_spmd.clone, body=%wide.wide.region_11.12_spmd.clone.sunk | while | flops 679871232 | bytes 27977976 | solution.py:292
  848.4 13.1 reduce-scatter.17.cloned.1.call-done
  875.3 20.3 %reduce-scatter.19.cloned.1.call-done = bf16[2,1,256,512]{3,2,0,1:T(8,128)(2,1)} async-done(((bf16[8,1,256,512]{3,2,0,1:T(8,128)(2,1)}), bf16[2,1,256,512]{3,2,0,1:T(8,128)(2,1)}) %reduce-scatter.19.cloned.1.call-update) | async-done | bytes 524304 | tf_op jit(solution)/shard_map/reduce_scatter | solution.py:299
  926.6 14.6 %bitcast_convert_fusion = bf16[2048,2,2048]{2,0,1:T(8,128)(2,1)} fusion(bf16[2,256,2048,1]{2,1,0,3:T(8,128)(2,1)S(1)} %bitcast.464, bf16[2,256,1,2048]{3,1,0,2:T(8,128)(2,1)} %copy-done.37, bf16[2,256,1,2048]{3,1,0,2:T(8,128)(2,1)} %copy-done.36), kind=kOutput, calls=%fused_computation.58 | convolution fusion | flops 8606711808 | bytes 23068672 | tf_op jit(solution)/shard_map/spcd,spctf->dtf/dot_general | solution.py:227
  943.1 27.3 %reduce-scatter.29.cloned.1.call-done = bf16[2048,256]{1,0:T(8,128)(2,1)} async-done(((bf16[2048,2048]{1,0:T(8,128)(2,1)}), bf16[2048,256]{1,0:T(8,128)(2,1)}) %reduce-scatter.29.cloned.1.call-update) | async-done | bytes 1048592 | tf_op jit(solution)/shard_map/reduce_scatter | solution.py:242
  973.1 41.6 %reduce-scatter.25.cloned.1.call-done = bf16[512,256]{1,0:T(8,128)(2,1)} async-done(((bf16[512,2048]{1,0:T(8,128)(2,1)}), bf16[512,256]{1,0:T(8,128)(2,1)}) %reduce-scatter.25.cloned.1.call-update) | async-done | bytes 262160 | tf_op jit(solution)/shard_map/reduce_scatter | solution.py:333
  1016.5 77.7 %reduce-scatter.21.cloned.1.call-done = f32[1,2,64,2048]{3,2,1,0:T(8,128)} async-done(((f32[1,2,256,2048]{3,2,1,0:T(8,128)}), f32[1,2,64,2048]{3,2,1,0:T(8,128)}) %reduce-scatter.21.cloned.1.call-update) | async-done | bytes 1048592 | tf_op jit(solution)/shard_map/reduce_scatter | solution.py:82
  1095.9 13.6 all-reduce.3
  1122.1 51.9 %reduce-scatter.13.cloned.1.call-done = f32[1,2,64,2048]{3,2,1,0:T(8,128)} async-done(((f32[1,2,256,2048]{3,2,1,0:T(8,128)}), f32[1,2,64,2048]{3,2,1,0:T(8,128)}) %reduce-scatter.13.cloned.1.call-update) | async-done | bytes 1048592 | tf_op jit(solution)/shard_map/reduce_scatter | solution.py:74
  1177.1 62.2 %reduce-scatter.23.cloned.1.call-done = bf16[256,3,512]{2,0,1:T(8,128)(2,1)} async-done(((bf16[2048,3,512]{2,0,1:T(8,128)(2,1)}), bf16[256,3,512]{2,0,1:T(8,128)(2,1)}) %reduce-scatter.23.cloned.1.call-update) | async-done | bytes 786448 | tf_op jit(solution)/shard_map/reduce_scatter | solution.py:330
  1241.8 117.2 %reduce-scatter.27.cloned.1.call-done = bf16[256,2,2048]{2,0,1:T(8,128)(2,1)} async-done(((bf16[2048,2,2048]{2,0,1:T(8,128)(2,1)}), bf16[256,2,2048]{2,0,1:T(8,128)(2,1)}) %reduce-scatter.27.cloned.1.call-update) | async-done | bytes 2097168 | tf_op jit(solution)/shard_map/reduce_scatter | solution.py:239
  (451 shorter events, 447.0 us)
Async XLA Ops:
  7.2 80.8 %all-gather.11.cloned.1.call-start = ((), (), s32[]{:S(2)}) async-start(), calls=%async_computation.10 | async-start | bytes 7077888 | tf_op jit(solution)/shard_map/all_gather | solution.py:143
  7.9 133.5 %all-gather.13.cloned.1.call-start = ((), (), s32[]{:S(2)}) async-start(), calls=%async_computation.11 | async-start | bytes 2621440 | tf_op jit(solution)/shard_map/all_gather | solution.py:164
  21.6 14.2 %collective-permute-start = (bf16[1,1,2,64,2048]{4,3,2,1,0:T(8,128)(2,1)S(1)}, bf16[1,1,2,64,2048]{4,3,2,1,0:T(8,128)(2,1)S(1)}, u32[]{:S(2)}, u32[]{:S(2)}) collective-permute-start(bf16[1,1,2,64,2048]{4,3,2,1,0:T(8,128)(2,1)S(1)} %get-tuple-element.492), channel_id=1, source_target_pairs={{0,1},{1,0},{2,3},{3,2},{4,5},{5,4},{6,7},{7,6},{8,9},{9,8},{10,11... | collective-permute-start | bytes 1572872 | tf_op jit(solution)/shard_map/ppermute | solution.py:29
  36.4 48.1 %collective-permute-start.1 = (bf16[2,1,2,64,2048]{4,3,2,0,1:T(8,128)(2,1)S(1)}, bf16[2,1,2,64,2048]{4,3,2,0,1:T(8,128)(2,1)}, u32[]{:S(2)}, u32[]{:S(2)}) collective-permute-start(bf16[2,1,2,64,2048]{4,3,2,0,1:T(8,128)(2,1)S(1)} %get-tuple-element.490), channel_id=1, source_target_pairs={{0,2},{1,3},{2,0},{3,1},{4,6},{5,7},{6,4},{7,5},{8,10},{9,11},{10,... | collective-permute-start | bytes 3145736 | tf_op jit(solution)/shard_map/ppermute | solution.py:29
  118.4 47.7 %all-gather.15.cloned.1.call-start = ((), (), s32[]{:S(2)}) async-start(), calls=%async_computation.12 | async-start | bytes 2621440 | tf_op jit(solution)/shard_map/all_gather | solution.py:165
  122.1 141.0 %all-gather.17.cloned.1.call-start = ((), (), s32[]{:S(2)}) async-start(), calls=%async_computation.13 | async-start | bytes 2359296 | tf_op jit(solution)/shard_map/all_gather | solution.py:144
  122.7 222.7 %reduce-scatter.11.cloned.1.call-start = ((), (), s32[]{:S(2)}) async-start(), calls=%async_computation.14 | async-start | bytes 5242880 | tf_op jit(solution)/shard_map/reduce_scatter | solution.py:74
  268.2 169.8 %all-gather.19.cloned.1.call-start = ((), (), s32[]{:S(2)}) async-start(), calls=%async_computation.15 | async-start | bytes 18874368 | tf_op jit(solution)/shard_map/all_gather | solution.py:200
  272.0 213.2 %all-gather.23.cloned.1.call-start = ((), (), s32[]{:S(2)}) async-start(), calls=%async_computation.18 | async-start | bytes 2621440 | tf_op jit(solution)/shard_map/all_gather | solution.py:78
  272.8 269.0 %all-gather.21.cloned.1.call-start = ((), (), s32[]{:S(2)}) async-start(), calls=%async_computation.16 | async-start | bytes 9437184 | tf_op jit(solution)/shard_map/all_gather | solution.py:201
  273.6 372.3 %reduce-scatter.15.cloned.1.call-start = ((), (), s32[]{:S(2)}) async-start(), calls=%async_computation.19 | async-start | bytes 5242880 | tf_op jit(solution)/shard_map/reduce_scatter | solution.py:82
  346.8 300.7 %copy-start.1 = (f32[1,2,64,2048]{3,2,1,0:T(8,128)}, f32[1,2,64,2048]{3,2,1,0:T(8,128)S(1)}, u32[]{:S(2)}) copy-start(f32[1,2,64,2048]{3,2,1,0:T(8,128)S(1)} %get-tuple-element.460) | copy-start | bytes 3145732
  347.0 13.4 collective-permute-start.2
  360.7 48.0 %collective-permute-start.3 = (bf16[2,1,2,64,2048]{4,3,2,0,1:T(8,128)(2,1)S(1)}, bf16[2,1,2,64,2048]{4,3,2,0,1:T(8,128)(2,1)S(1)}, u32[]{:S(2)}, u32[]{:S(2)}) collective-permute-start(bf16[2,1,2,64,2048]{4,3,2,0,1:T(8,128)(2,1)S(1)} %get-tuple-element.484), channel_id=1, source_target_pairs={{0,2},{1,3},{2,0},{3,1},{4,6},{5,7},{6,4},{7,5},{8,10},{9,11},{10,... | collective-permute-start | bytes 3145736 | tf_op jit(solution)/shard_map/ppermute | solution.py:29
  568.9 126.1 %all-gather.25.cloned.1.call-start = ((), (), s32[]{:S(2)}) async-start(), calls=%async_computation.20 | async-start | bytes 2621440 | tf_op jit(solution)/shard_map/all_gather | solution.py:78
  648.7 212.8 %reduce-scatter.17.cloned.1.call-start = ((), (), s32[]{:S(2)}) async-start(), calls=%async_computation.21 | async-start | bytes 2621440 | tf_op jit(solution)/shard_map/reduce_scatter | solution.py:296
  831.3 64.3 %reduce-scatter.19.cloned.1.call-start = ((), (), s32[]{:S(2)}) async-start(), calls=%async_computation.22 | async-start | bytes 2621440 | tf_op jit(solution)/shard_map/reduce_scatter | solution.py:299
  831.9 138.5 %reduce-scatter.29.cloned.1.call-start = ((), (), s32[]{:S(2)}) async-start(), calls=%async_computation.27 | async-start | bytes 9437184 | tf_op jit(solution)/shard_map/reduce_scatter | solution.py:242
  841.3 173.4 %reduce-scatter.25.cloned.1.call-start = ((), (), s32[]{:S(2)}) async-start(), calls=%async_computation.25 | async-start | bytes 2359296 | tf_op jit(solution)/shard_map/reduce_scatter | solution.py:333
  845.6 248.6 %reduce-scatter.21.cloned.1.call-start = ((), (), s32[]{:S(2)}) async-start(), calls=%async_computation.23 | async-start | bytes 5242880 | tf_op jit(solution)/shard_map/reduce_scatter | solution.py:82
  904.2 269.7 %reduce-scatter.13.cloned.1.call-start = ((), (), s32[]{:S(2)}) async-start(), calls=%async_computation.17 | async-start | bytes 5242880 | tf_op jit(solution)/shard_map/reduce_scatter | solution.py:74
  916.9 322.4 %reduce-scatter.23.cloned.1.call-start = ((), (), s32[]{:S(2)}) async-start(), calls=%async_computation.24 | async-start | bytes 7077888 | tf_op jit(solution)/shard_map/reduce_scatter | solution.py:330
  925.1 434.0 %reduce-scatter.27.cloned.1.call-start = ((), (), s32[]{:S(2)}) async-start(), calls=%async_computation.26 | async-start | bytes 18874368 | tf_op jit(solution)/shard_map/reduce_scatter | solution.py:239
  943.1 230.9 %copy-start.2 = (f32[1,2,64,2048]{3,2,1,0:T(8,128)S(1)}, f32[1,2,64,2048]{3,2,1,0:T(8,128)}, u32[]{:S(2)}) copy-start(f32[1,2,64,2048]{3,2,1,0:T(8,128)} %copy-done.1) | copy-start | bytes 3145732
  (43 other events, 1412.1 us)
Sparse Core Ops, SparseCore 0:
  9.9 48.1 all-gather.10
  118.6 22.7 all-gather.12
  143.5 22.5 all-gather.14
  167.8 28.0 all-gather.16
  268.3 77.0 reduce-scatter.10
  347.7 90.2 all-gather.18
  439.5 45.6 all-gather.22
  487.1 54.6 all-gather.20
  569.0 76.7 reduce-scatter.14
  648.8 46.1 all-gather.24
  831.4 29.9 reduce-scatter.16
  864.4 31.1 reduce-scatter.18
  899.1 71.2 reduce-scatter.28
  973.5 41.1 reduce-scatter.24
  1017.4 76.7 reduce-scatter.20
  1096.4 77.5 reduce-scatter.12
  1177.2 62.0 reduce-scatter.22
  1242.8 116.2 reduce-scatter.26
